TPU v7x, 32 devices: a whole 2x2x4 slice. The times are simulated.
32 devices in a mesh: band: 8 (over z, x), sub: 4 (over y, core).
Axes of the slice: x: 2, y: 2, z: 4, core: 2. Of those that a mesh axis runs over, the one named last changes fastest.
Arguments:
- grad_pred: bfloat16 [227, 24576], P(None, ('band', 'sub')), may hold values from -6 to 6
- grid_latent: bfloat16 [24576, 512], P(('band', 'sub')), may hold values from -6 to 6
- mesh_latent: bfloat16 [10240, 512], P(('band', 'sub')), may hold values from -6 to 6
- send_slot: int32 [24576], P(('band', 'sub')), may hold values from 0 to 2303, as said below
- edge_src: int32 [3, 73728], P(None, ('band', 'sub')), may hold values from 0 to 10239, as said below
- w_mesh: bfloat16 [512, 512], replicated, may hold values from -0.25 to 0.25
- w_grid: bfloat16 [512, 512], replicated, may hold values from -0.25 to 0.25
- w_msg: bfloat16 [512, 512], replicated, may hold values from -0.25 to 0.25
- w_out: bfloat16 [512, 227], replicated, may hold values from -0.25 to 0.25
Outputs:
- mesh_grad: bfloat16 [10240, 512], P(('band', 'sub'))
- grad_w_mesh: float32 [512, 512], replicated
- grad_w_grid: float32 [512, 512], replicated
- grad_w_msg: float32 [512, 512], replicated
- grad_w_out: float32 [512, 227], replicated
Inputs may be any that keep to these rules, and one draw needn't show every extreme that they name: For grid point p on latitude-major device i, send_slot[p] = j * 72 + r names patch-major device j and a rank r. On one device i the values are distinct, and for each j the ranks used are 0 to the count of i's points sent to j minus 1. Every such count is at most 72, and 72 is reached in every draw. Every grid point thereby gets one patch-major slot; live slots of each source stand at the front of its block of 72. One patch-major device holds at most 1920 live slots, reached on some device in every draw. `edge_src`: A slot on patch-major device j, of band b = j // 4, names senders in patch b only: mesh rows b * 1280 to (b + 1) * 1280 - 1. Entries of empty slots lie in that range too and are not read.
All inputs are finite; a program needn't handle non-finite values.
Results may differ from a plain program's by a relative error of at most 0.0076.
Values may be sent and summed in bfloat16 or wider, within the bound.
A program may use at most 128 MiB of HBM per device.

v0:
```python
import functools
import math

import jax
import jax.numpy as jnp
from jax import lax
from jax.experimental import pallas as pl
from jax.experimental.pallas import tpu as pltpu
from jax.sharding import PartitionSpec as P

HALVES = 2
LANES = 128
TILE = 16


def latitude_weight(points, total):
    angle = jnp.pi * ((points.astype(jnp.float32) + 0.5) / total - 0.5)
    return 0.5 * jnp.pi * jnp.cos(angle)


def contract_rows(left, right):
    return lax.dot_general(
        left, right, (((0,), (0,)), ((), ())), preferred_element_type=jnp.float32
    )


def times_transpose(left, right):
    return lax.dot_general(
        left, right, (((1,), (1,)), ((), ())), preferred_element_type=jnp.float32
    )


def times(left, right):
    return jnp.dot(left, right, preferred_element_type=jnp.float32)


def round_up(value, multiple):
    return -(-value // multiple) * multiple


def remote(src, dst, send_sem, recv_sem, band, sub):
    return pltpu.make_async_remote_copy(
        src_ref=src,
        dst_ref=dst,
        send_sem=send_sem,
        recv_sem=recv_sem,
        device_id=(band, sub),
        device_id_type=pl.DeviceIdType.MESH,
    )


def greet(band, sub):
    pl.semaphore_signal(
        pltpu.get_barrier_semaphore(),
        inc=1,
        device_id=(band, sub),
        device_id_type=pl.DeviceIdType.MESH,
    )


def edge_kernel(
    bands,
    subs,
    capacity,
    slot_ref,
    latent_ref,
    weighted_ref,
    block_ref,
    edge_ref,
    w_mesh_ref,
    w_grid_ref,
    w_msg_ref,
    w_out_ref,
    node_ref,
    parts_ref,
    rows_out,
    grads_out,
    rows_in,
    grads_in,
    table,
    proj,
    edge_in,
    index_cols,
    act_weight,
    hot,
    pre,
    grid_part,
    act_grad,
    act_sum,
    pre_grad,
    grid_grad,
    node_acc,
    grid_acc,
    out_acc,
    rows_send,
    rows_recv,
    grads_send,
    grads_recv,
    half_send,
    pair_send,
    twin_send,
    table_recv,
    edge_send,
    edge_recv,
):
    lows = bands // HALVES
    pairs = subs // 2
    padded = rows_out.shape[2]
    used = subs * capacity
    block_rows, width = block_ref.shape
    patch = subs * block_rows
    points = latent_ref.shape[0]
    band, sub = lax.axis_index("band"), lax.axis_index("sub")
    half, low = band // lows, band % lows
    pair, parity = sub // 2, sub % 2
    twin = 2 * pair + 1 - parity
    group = HALVES * subs
    mine = half * subs + sub

    def low_ahead(step):
        return (low // 2 + step // 2) % (lows // 2) * 2 + (low % 2 + step % 2) % 2

    def low_behind(step):
        return (low // 2 + lows // 2 - step // 2) % (lows // 2) * 2 + (low % 2 + step % 2) % 2

    def member(step):
        index = (mine + step) % group
        return index // subs, index % subs

    @pl.loop(1, group)
    def _(step):
        other_half, other_sub = member(step)
        greet(other_half * lows + low, other_sub)

    @pl.loop(1, lows)
    def _(step):
        greet(half * lows + low_ahead(step), sub)

    pl.semaphore_wait(pltpu.get_barrier_semaphore(), group - 1 + lows - 1)

    def half_copy(source, target):
        return remote(
            block_ref,
            table.at[source, sub],
            half_send.at[target],
            table_recv.at[source, sub],
            target * lows + low,
            sub,
        )

    def pair_copy(src, source_half, source, target):
        place = 2 * source + parity
        return remote(
            src,
            table.at[source_half, place],
            pair_send.at[source_half, target],
            table_recv.at[source_half, place],
            band,
            2 * target + parity,
        )

    def twin_copy(src, source_half, source):
        return remote(
            src,
            table.at[source_half, source],
            twin_send.at[source_half, source // 2],
            table_recv.at[source_half, source],
            band,
            twin,
        )

    def edge_copy(from_half, from_sub, to_half, to_sub):
        return remote(
            edge_ref.at[to_half, to_sub],
            edge_in.at[from_half, from_sub],
            edge_send.at[to_half, to_sub],
            edge_recv.at[from_half, from_sub],
            to_half * lows + low,
            to_sub,
        )

    for step in range(1, HALVES):
        half_copy(half, (half + step) % HALVES).start()
    for step in range(1, pairs):
        pair_copy(block_ref, half, pair, (pair + step) % pairs).start()
    twin_copy(block_ref, half, sub).start()

    @pl.loop(1, group)
    def _(step):
        other_half, other_sub = member(step)
        edge_copy(half, sub, other_half, other_sub).start()

    def spread(target, rows, grads):
        for part in range(HALVES):
            places = lax.broadcasted_iota(jnp.int32, (padded, points), 0)
            places = places + (target * HALVES + part) * padded
            one_hot = jnp.where(places == slot_ref[...], 1.0, 0.0).astype(jnp.bfloat16)
            rows[part] = times(one_hot, latent_ref[...]).astype(jnp.bfloat16)
            grads[part] = times_transpose(one_hot, weighted_ref[...]).astype(jnp.bfloat16)

    def rows_copy(source, target):
        return remote(
            rows_out.at[target],
            rows_in.at[source],
            rows_send.at[target],
            rows_recv.at[source],
            half * lows + target,
            sub,
        )

    def grads_copy(source, target):
        return remote(
            grads_out.at[target],
            grads_in.at[source],
            grads_send.at[target],
            grads_recv.at[source],
            half * lows + target,
            sub,
        )

    @pl.loop(1, lows)
    def _(step):
        target = low_ahead(step)
        spread(target, rows_out.at[target], grads_out.at[target])
        rows_copy(low, target).start()
        grads_copy(low, target).start()

    spread(low, rows_in.at[low], grads_in.at[low])

    table[half, sub] = block_ref[...]
    edge_in[half, sub] = edge_ref[half, sub]
    act_weight[...] = lax.dot_general(
        w_out_ref[...], w_msg_ref[...], (((0,), (1,)), ((), ())), preferred_element_type=jnp.float32
    ).astype(jnp.bfloat16)
    node_acc[...] = jnp.zeros_like(node_acc)
    grid_acc[...] = jnp.zeros_like(grid_acc)
    out_acc[...] = jnp.zeros_like(out_acc)

    def arrived(source_half, source):
        return remote(
            block_ref,
            table.at[source_half, source],
            twin_send.at[0, 0],
            table_recv.at[source_half, source],
            band,
            twin,
        ).wait_recv

    def project(source_half, source):
        rows = pl.ds(pl.multiple_of(source * block_rows, block_rows), block_rows)
        proj[source_half, rows] = times(table[source_half, source], w_mesh_ref[...]).astype(
            jnp.bfloat16
        )

    project(half, sub)
    for step in range(1, pairs):
        source = 2 * ((pair + step) % pairs) + parity
        arrived(half, source)()
        twin_copy(table.at[half, source], half, source).start()
        project(half, source)
    for step in range(1, HALVES):
        source_half = (half + step) % HALVES
        arrived(source_half, sub)()
        place = table.at[source_half, sub]
        twin_copy(place, source_half, sub).start()
        for other in range(1, pairs):
            pair_copy(place, source_half, pair, (pair + other) % pairs).start()
        project(source_half, sub)
    for source_pair in range(pairs):
        source = 2 * source_pair + 1 - parity
        arrived(half, source)()
        project(half, source)
    for step in range(1, HALVES):
        source_half = (half + step) % HALVES
        for other in range(1, pairs):
            source = 2 * ((pair + other) % pairs) + parity
            arrived(source_half, source)()
            twin_copy(table.at[source_half, source], source_half, source).start()
            project(source_half, source)
        for source_pair in range(pairs):
            source = 2 * source_pair + 1 - parity
            arrived(source_half, source)()
            project(source_half, source)

    @pl.loop(1, group)
    def _(step):
        other_half, other_sub = member(step)
        edge_copy(other_half, other_sub, half, sub).wait_recv()

    lanes = index_cols.shape[2]
    count = edge_ref.shape[2]
    for part in range(HALVES):
        total = jnp.zeros((count, lanes), jnp.int32)
        for source in range(subs):
            piece = edge_in[part, source]
            if lanes > LANES:
                piece = jnp.concatenate(
                    [piece, jnp.zeros((count, lanes - LANES), jnp.int32)], axis=1
                )
            if source:
                piece = pltpu.roll(piece, source * capacity, 1)
            total = total + piece
        if count < LANES:
            total = jnp.concatenate([total, jnp.zeros((LANES - count, lanes), jnp.int32)], axis=0)
        flipped = total.T
        for source in range(lows):
            moved = pltpu.roll(flipped, LANES - 3 * source, 1) if source else flipped
            index_cols[source, part] = moved

    def process(source):
        for part in range(HALVES):
            for corner in range(3):
                column = index_cols[source, part, 0:padded, corner : corner + 1]
                nodes = lax.broadcasted_iota(jnp.int32, (padded, patch), 1)
                hot[corner * padded : (corner + 1) * padded, :] = jnp.where(
                    nodes == column, 1.0, 0.0
                ).astype(jnp.bfloat16)
            pre[...] = times(hot[...], proj[part])
            grid_part[...] = times(rows_in[source, part], w_grid_ref[...]).astype(jnp.bfloat16)
            act_grad[...] = times(grads_in[source, part], act_weight[...])

            @pl.loop(0, padded // TILE)
            def _(tile):
                start = pl.multiple_of(tile * TILE, TILE)
                rows = pl.ds(start, TILE)
                base = grid_part[rows].astype(jnp.float32)
                upper = act_grad[rows]
                acts, grads = None, None
                for corner in range(3):
                    place = pl.ds(pl.multiple_of(corner * padded + start, TILE), TILE)
                    value = pre[place] + base
                    sigma = 0.5 * jnp.tanh(0.5 * value) + 0.5
                    act = value * sigma
                    grad = (upper * (sigma + act * (1.0 - sigma))).astype(jnp.bfloat16)
                    pre_grad[place] = grad
                    grad = grad.astype(jnp.float32)
                    acts = act if acts is None else acts + act
                    grads = grad if grads is None else grads + grad
                act_sum[rows] = acts.astype(jnp.bfloat16)
                grid_grad[rows] = grads.astype(jnp.bfloat16)

            out_acc[...] += contract_rows(act_sum[...], grads_in[source, part])
            grid_acc[...] += contract_rows(rows_in[source, part], grid_grad[...])
            node_acc[part] += contract_rows(hot[...], pre_grad[...])

    @pl.loop(0, lows)
    def _(step):
        source = low_behind(step)

        @pl.when(step > 0)
        def _():
            rows_copy(source, source).wait_recv()
            grads_copy(source, source).wait_recv()

        process(source)

    mesh_total = None
    for part in range(HALVES):
        for source in range(subs):
            rows = pl.ds(source * block_rows, block_rows)
            value = node_acc[part, rows].astype(jnp.bfloat16)
            node_ref[part, source] = value
            term = contract_rows(table[part, source], value)
            mesh_total = term if mesh_total is None else mesh_total + term
    parts_ref[:, 0:width] = mesh_total.astype(jnp.bfloat16)
    parts_ref[:, width : 2 * width] = grid_acc[...].astype(jnp.bfloat16)
    parts_ref[:, 2 * width :] = out_acc[...].astype(jnp.bfloat16)

    @pl.loop(1, lows)
    def _(step):
        target = low_ahead(step)
        rows_copy(low, target).wait_send()
        grads_copy(low, target).wait_send()

    for step in range(1, HALVES):
        half_copy(half, (half + step) % HALVES).wait_send()
    for source_half in range(HALVES):
        for step in range(1, pairs):
            pair_copy(block_ref, source_half, pair, (pair + step) % pairs).wait_send()
        for source_pair in range(pairs):
            twin_copy(block_ref, source_half, 2 * source_pair + parity).wait_send()

    @pl.loop(1, group)
    def _(step):
        other_half, other_sub = member(step)
        edge_copy(half, sub, other_half, other_sub).wait_send()


def edge_pass(slots, latent, weighted, block, edges, w_mesh, w_grid, w_msg, w_out, capacity):
    bands, subs = lax.axis_size("band"), lax.axis_size("sub")
    lows, pairs = bands // HALVES, subs // 2
    padded = round_up(subs * capacity, TILE)
    block_rows, width = block.shape
    patch = subs * block_rows
    columns = weighted.shape[0]
    lanes = round_up(padded, LANES)
    vmem = pl.BlockSpec(memory_space=pltpu.VMEM)
    dma = pltpu.SemaphoreType.DMA
    half, full = jnp.bfloat16, jnp.float32
    return pl.pallas_call(
        functools.partial(edge_kernel, bands, subs, capacity),
        out_shape=(
            jax.ShapeDtypeStruct((HALVES, subs, block_rows, width), half),
            jax.ShapeDtypeStruct((width, 2 * width + columns), half),
        ),
        in_specs=[vmem] * 9,
        out_specs=(vmem, vmem),
        scratch_shapes=[
            pltpu.VMEM((lows, HALVES, padded, width), half),
            pltpu.VMEM((lows, HALVES, padded, columns), half),
            pltpu.VMEM((lows, HALVES, padded, width), half),
            pltpu.VMEM((lows, HALVES, padded, columns), half),
            pltpu.VMEM((HALVES, subs, block_rows, width), half),
            pltpu.VMEM((HALVES, patch, width), half),
            pltpu.VMEM(edges.shape, jnp.int32),
            pltpu.VMEM((lows, HALVES, lanes, LANES), jnp.int32),
            pltpu.VMEM((columns, width), half),
            pltpu.VMEM((3 * padded, patch), half),
            pltpu.VMEM((3 * padded, width), full),
            pltpu.VMEM((padded, width), half),
            pltpu.VMEM((padded, width), full),
            pltpu.VMEM((padded, width), half),
            pltpu.VMEM((3 * padded, width), half),
            pltpu.VMEM((padded, width), half),
            pltpu.VMEM((HALVES, patch, width), full),
            pltpu.VMEM((width, width), full),
            pltpu.VMEM((width, columns), full),
        ]
        + [dma((lows,))] * 4
        + [
            dma((HALVES,)),
            dma((HALVES, pairs)),
            dma((HALVES, pairs)),
            dma((HALVES, subs)),
            dma((HALVES, subs)),
            dma((HALVES, subs)),
        ],
        compiler_params=pltpu.CompilerParams(
            collective_id=1, has_side_effects=True, vmem_limit_bytes=64000000
        ),
    )(slots, latent, weighted, block, edges, w_mesh, w_grid, w_msg, w_out)


def reduce_kernel(
    subs,
    parts_ref,
    nodes_ref,
    total_ref,
    node_ref,
    half_in,
    half_sum,
    group_in,
    node_in,
    node_sum,
    node_last,
    node_half,
    node_far,
    half_sem,
    group_send,
    group_recv,
    own_send,
    own_recv,
    pass_send,
    pass_recv,
    node_send,
    node_recv,
    last_send,
    last_recv,
    far_send,
    far_recv,
):
    devices = parts_ref.shape[0]
    groups = devices // 2
    sub_groups = subs // 2
    lows = devices // subs // HALVES
    band, sub = lax.axis_index("band"), lax.axis_index("sub")
    me = band * subs + sub
    own_half, low = band // lows, band % lows
    parity, group = me % 2, me // 2
    other = 1 - parity
    partner = me + 1 - 2 * parity
    own_pair = sub // 2

    def to_device(src, dst, send_sem, recv_sem, device):
        return remote(src, dst, send_sem, recv_sem, device // subs, device % subs)

    def member(index):
        return 2 * index + parity

    def ahead(step):
        return (group + step) % groups

    def behind(step):
        return (group + groups - step) % groups

    greet(partner // subs, partner % subs)

    @pl.loop(1, groups)
    def _(step):
        device = member(ahead(step))
        greet(device // subs, device % subs)

    pl.semaphore_wait(pltpu.get_barrier_semaphore(), groups)

    node_copies = [
        to_device(
            nodes_ref.at[part, 2 * pair + other],
            node_in.at[part, pair],
            node_send.at[part, pair],
            node_recv.at[part, pair],
            partner,
        )
        for part in range(HALVES)
        for pair in range(sub_groups)
    ]
    for copy in node_copies:
        copy.start()
    half_copy = to_device(
        parts_ref.at[pl.ds(other * groups, groups)], half_in, half_sem.at[0], half_sem.at[1], partner
    )
    half_copy.start()
    for copy in node_copies:
        copy.wait()

    def last_copy(part, source, target):
        return to_device(
            node_sum.at[part, target],
            node_last.at[part, source],
            last_send.at[part, target],
            last_recv.at[part, source],
            band * subs + 2 * target + parity,
        )

    def add_node(part, pair):
        return nodes_ref[part, 2 * pair + parity].astype(jnp.float32) + node_in[part, pair].astype(
            jnp.float32
        )

    for turn in range(HALVES):
        part = (own_half + 1 + turn) % HALVES
        for step in range(1, sub_groups):
            target = (own_pair + step) % sub_groups
            node_sum[part, target] = add_node(part, target).astype(node_sum.dtype)
            last_copy(part, own_pair, target).start()

    half_copy.wait()

    def add_half(index):
        return parts_ref[parity * groups + index].astype(jnp.float32) + half_in[index].astype(
            jnp.float32
        )

    def group_copy(source, target):
        return to_device(
            half_sum.at[target],
            group_in.at[source],
            group_send.at[target],
            group_recv.at[source],
            member(target),
        )

    @pl.loop(1, groups)
    def _(step):
        target = ahead(step)
        half_sum[target] = add_half(target).astype(half_sum.dtype)
        group_copy(group, target).start()

    def far_copy(source, target):
        return to_device(
            node_half.at[target],
            node_far.at[source],
            far_send.at[target],
            far_recv.at[source],
            (target * lows + low) * subs + sub,
        )

    def gather_node(part):
        running = add_node(part, own_pair)
        for step in range(1, sub_groups):
            source = (own_pair + sub_groups - step) % sub_groups
            last_copy(part, source, source).wait_recv()
            running = running + node_last[part, source].astype(jnp.float32)
        return running

    for step in range(1, HALVES):
        target = (own_half + step) % HALVES
        node_half[target] = gather_node(target).astype(node_half.dtype)
        far_copy(own_half, target).start()

    def take(step, running):
        source = behind(step)
        group_copy(source, source).wait_recv()
        return running + group_in[source].astype(jnp.float32)

    mine = parity * groups + group
    total_ref[mine] = lax.fori_loop(1, groups, take, add_half(group)).astype(total_ref.dtype)

    def own_copy(source, target):
        place = total_ref.at[parity * groups + source]
        return to_device(place, place, own_send.at[target], own_recv.at[source], member(target))

    def pass_copy(source, half):
        place = total_ref.at[half * groups + source]
        return to_device(place, place, pass_send.at[source], pass_recv.at[source], partner)

    @pl.loop(1, groups)
    def _(step):
        own_copy(group, ahead(step)).start()

    pass_copy(group, parity).start()

    running = gather_node(own_half)
    for step in range(1, HALVES):
        source = (own_half + HALVES - step) % HALVES
        far_copy(source, source).wait_recv()
        running = running + node_far[source].astype(jnp.float32)
    node_ref[...] = running.astype(node_ref.dtype)

    @pl.loop(1, groups)
    def _(step):
        source = behind(step)
        own_copy(source, source).wait_recv()
        pass_copy(source, parity).start()

    @pl.loop(0, groups)
    def _(step):
        source = ahead(step)
        pass_copy(source, other).wait_recv()
        pass_copy(source, parity).wait_send()

    @pl.loop(1, groups)
    def _(step):
        target = ahead(step)
        group_copy(group, target).wait_send()
        own_copy(group, target).wait_send()

    for part in range(HALVES):
        for step in range(1, sub_groups):
            last_copy(part, own_pair, (own_pair + step) % sub_groups).wait_send()
    for step in range(1, HALVES):
        far_copy(own_half, (own_half + step) % HALVES).wait_send()


def reduce_all(parts, nodes):
    devices, rows, columns = parts.shape
    _, subs, node_rows, width = nodes.shape
    groups, sub_groups = devices // 2, subs // 2
    vmem = pl.BlockSpec(memory_space=pltpu.VMEM)
    dma = pltpu.SemaphoreType.DMA
    return pl.pallas_call(
        functools.partial(reduce_kernel, subs),
        out_shape=(
            jax.ShapeDtypeStruct(parts.shape, parts.dtype),
            jax.ShapeDtypeStruct((node_rows, width), nodes.dtype),
        ),
        in_specs=[vmem, vmem],
        out_specs=(vmem, vmem),
        scratch_shapes=[pltpu.VMEM((groups, rows, columns), parts.dtype)] * 3
        + [pltpu.VMEM((HALVES, sub_groups, node_rows, width), nodes.dtype)] * 3
        + [pltpu.VMEM((HALVES, node_rows, width), nodes.dtype)] * 2
        + [dma((2,))]
        + [dma((groups,))] * 6
        + [dma((HALVES, sub_groups))] * 4
        + [dma((HALVES,))] * 2,
        compiler_params=pltpu.CompilerParams(collective_id=0, has_side_effects=True),
    )(parts, nodes)


def shards(grad_pred, grid_latent, mesh_latent, send_slot, edge_src, w_mesh, w_grid, w_msg, w_out):
    both = ("band", "sub")
    grid_rows, width = grid_latent.shape
    channels = grad_pred.shape[0]
    bands, subs = lax.axis_size("band"), lax.axis_size("sub")
    devices = bands * subs
    lows = bands // HALVES
    block_rows = mesh_latent.shape[0]
    capacity = 3 * grid_rows // devices
    padded = round_up(subs * capacity, TILE)
    total_points = grid_rows * devices
    own_index = lax.axis_index(both)
    points = own_index * grid_rows + jnp.arange(grid_rows, dtype=jnp.int32)
    weighted = (
        latitude_weight(points, total_points)[None, :] * grad_pred.astype(jnp.float32)
    ).astype(jnp.bfloat16)
    padding = -channels % LANES
    weighted = jnp.pad(weighted, ((0, padding), (0, 0)))
    w_out = jnp.pad(w_out, ((0, 0), (0, padding)))
    holder, rank = send_slot // capacity, send_slot % capacity
    holder_band, holder_sub = holder // subs, holder % subs
    holder_half, holder_low = holder_band // lows, holder_band % lows
    slots = (holder_low * HALVES + holder_half) * padded + holder_sub * capacity + rank
    local = edge_src - lax.axis_index("band") * (subs * block_rows)
    local = local.reshape(3, HALVES, lows, subs, capacity).transpose(1, 3, 2, 0, 4)
    local = local.reshape(HALVES, subs, 3 * lows, capacity)
    local = jnp.pad(local, ((0, 0), (0, 0), (0, -3 * lows % 8), (0, LANES - capacity)))
    nodes, parts = edge_pass(
        slots[None, :],
        grid_latent,
        weighted,
        mesh_latent,
        local,
        w_mesh,
        w_grid,
        w_msg,
        w_out,
        capacity,
    )
    totals, mesh_proj_grad = reduce_all(
        parts.reshape(devices, width // devices, parts.shape[1]), nodes
    )
    totals = totals.reshape(parts.shape)
    mesh_grad = times_transpose(mesh_proj_grad, w_mesh).astype(jnp.bfloat16)
    grad_scale = 1.0 / math.sqrt(3.0 * total_points)
    outer = totals[:, 2 * width :]
    return (
        mesh_grad,
        totals[:, :width].astype(jnp.float32) * grad_scale,
        totals[:, width : 2 * width].astype(jnp.float32) * grad_scale,
        times_transpose(outer, w_out) * grad_scale,
        contract_rows(w_msg, outer[:, :channels]) * grad_scale,
    )


def solution(mesh):
    placed = (
        P(None, ("band", "sub")),
        P(("band", "sub"), None),
        P(("band", "sub"), None),
        P(("band", "sub")),
        P(None, ("band", "sub")),
        P(),
        P(),
        P(),
        P(),
    )
    return jax.shard_map(
        shards,
        mesh=mesh,
        in_specs=placed,
        out_specs=(P(("band", "sub"), None), P(), P(), P(), P()),
        check_vma=False,
    )
```

profile of v0, /device:TPU:15, one launch (start us, length us, event | category | flops | bytes accessed | tf_op | source)
XLA Modules:
  0.0 147.1 jit_solution(16931967708380263151)
XLA Ops:
  0.6 0.0 copy-start.3
  0.7 0.8 fusion.7
  1.5 0.6 broadcast_in_dim.4.slot_ref
  2.0 0.8 broadcast_subtract_fusion
  2.8 0.1 reshape.33
  3.0 0.6 pad.13.edge_ref
  3.6 1.1 copy.18
  4.7 0.7 pad.14.w_out_ref
  5.4 0.0 copy-done.3
  5.4 0.1 multiply_convert_fusion
  5.5 0.8 pad.12.weighted_ref
  6.3 68.6 %shard_map.128 = (bf16[2,4,320,512]{3,2,1,0:T(8,128)(2,1)}, bf16[512,1280]{1,0:T(8,128)(2,1)}) custom-call(s32[1,768]{1,0:T(1,128)} %broadcast_in_dim.4.slot_ref, bf16[768,512]{1,0:T(8,128)(2,1)} %latent_ref.1, bf16[256,768]{1,0:T(8,128)(2,1)} %pad.12.weighted_ref, bf16[320,512]{1,0:T(8,128)(2,1)} %block_ref.1, s32[2,4,16,128]{3,2,1,0:T(8,128)} %pad.13.edge_ref, ...), custom_call_target="tpu_custom_call" | custom-call | tf_op jit(solution)/shard_map/pallas_call | solution.py:400
  74.9 0.0 copy-start
  74.9 65.0 %shard_map.129 = (bf16[32,16,1280]{2,1,0:T(8,128)(2,1)}, bf16[320,512]{1,0:T(8,128)(2,1)}) custom-call(bf16[32,16,1280]{2,1,0:T(8,128)(2,1)} %bitcast.13, bf16[2,4,320,512]{3,2,1,0:T(8,128)(2,1)} %get-tuple-element.10.nodes_ref), custom_call_target="tpu_custom_call" | custom-call | tf_op jit(solution)/shard_map/pallas_call | solution.py:650
  139.9 0.0 copy-start.1
  139.9 0.0 copy-start.2
  139.9 0.0 copy-done
  139.9 2.2 %convolution_convert_fusion = bf16[320,512]{1,0:T(8,128)(2,1)} fusion(bf16[320,512]{1,0:T(8,128)(2,1)} %get-tuple-element.11, bf16[512,512]{1,0:T(8,128)(2,1)S(1)} %copy-done), kind=kOutput, calls=%fused_computation.1 | convolution fusion | flops 167936000 | bytes 1179648 | tf_op jit(solution)/shard_map/dot_general | solution.py:28
  142.1 0.0 copy-done.1
  142.1 2.0 %fusion = f32[512,227]{0,1:T(8,128)} fusion(bf16[512,512]{1,0:T(8,128)(2,1)S(1)} %copy-done.1, bf16[512,1280]{1,0:T(8,128)(2,1)} %bitcast.10), kind=kOutput, calls=%fused_computation.3 | convolution fusion | flops 119129600 | bytes 1251328 | tf_op jit(solution)/shard_map/dot_general | solution.py:22
  144.2 0.0 copy-done.2
  144.2 1.3 convolution_multiply_fusion
  145.5 1.6 %convert_multiply_fusion = (f32[512,512]{1,0:T(8,128)}, f32[512,512]{1,0:T(8,128)}) fusion(bf16[512,1280]{1,0:T(8,128)(2,1)S(1)} %bitcast.12), kind=kLoop, calls=%fused_computation.4 | loop fusion | flops 1048576 | bytes 3145728 | tf_op jit(solution)/shard_map/mul | solution.py:718
  (3 shorter events, 0.1 us)
Async XLA Ops:
  0.6 4.8 %copy-start.3 = (bf16[227,768]{1,0:T(8,128)(2,1)S(1)}, bf16[227,768]{1,0:T(8,128)(2,1)}, u32[]{:S(2)}) copy-start(bf16[227,768]{1,0:T(8,128)(2,1)} %param.9) | copy-start | bytes 1046020
  74.9 65.1 %copy-start = (bf16[512,512]{1,0:T(8,128)(2,1)S(1)}, bf16[512,512]{1,0:T(8,128)(2,1)}, u32[]{:S(2)}) copy-start(bf16[512,512]{1,0:T(8,128)(2,1)} %w_mesh_ref.1) | copy-start | bytes 1572868
  139.9 2.2 %copy-start.1 = (bf16[512,512]{1,0:T(8,128)(2,1)S(1)}, bf16[512,512]{1,0:T(8,128)(2,1)}, u32[]{:S(2)}) copy-start(bf16[512,512]{1,0:T(8,128)(2,1)} %w_msg_ref.1) | copy-start | bytes 1572868
  139.9 4.3 %copy-start.2 = (bf16[32,16,1280]{2,1,0:T(8,128)(2,1)S(1)}, bf16[32,16,1280]{2,1,0:T(8,128)(2,1)}, u32[]{:S(2)}) copy-start(bf16[32,16,1280]{2,1,0:T(8,128)(2,1)} %get-tuple-element.12) | copy-start | bytes 3932164
where the time goes:
time: 147 us
  Pallas kernels  134 us (91%)
  matrix products  5.52 us (4%)
  local copies, waits for them, and re-layouts  3.98 us (3%)
  other arithmetic  3.24 us (2%)
    pallas_call x1, Pallas kernels, edge_pass(): pl.pallas_call(functools.partial(edge_kernel, bands, subs, capacity), out...  68.6 us
    pallas_call x1, Pallas kernels, reduce_all(): pl.pallas_call(functools.partial(reduce_kernel, subs), out_shape=(jax.Sha...  65 us
    dot_general x2, matrix products, times_transpose(): lax.dot_general(left, right, (((1,), (1,)), ((), ())), preferred_element_...  3.49 us

commit v1 on v0

v1 whole, which is shorter than its diff:
```python
import functools
import math

import jax
import jax.numpy as jnp
from jax import lax
from jax.experimental import pallas as pl
from jax.experimental.pallas import tpu as pltpu
from jax.sharding import PartitionSpec as P

HALVES = 2
LANES = 128
TILE = 16


def latitude_weight(points, total):
    angle = jnp.pi * ((points.astype(jnp.float32) + 0.5) / total - 0.5)
    return 0.5 * jnp.pi * jnp.cos(angle)


def contract_rows(left, right):
    return lax.dot_general(
        left, right, (((0,), (0,)), ((), ())), preferred_element_type=jnp.float32
    )


def times_transpose(left, right):
    return lax.dot_general(
        left, right, (((1,), (1,)), ((), ())), preferred_element_type=jnp.float32
    )


def times(left, right):
    return jnp.dot(left, right, preferred_element_type=jnp.float32)


def round_up(value, multiple):
    return -(-value // multiple) * multiple


def remote(src, dst, send_sem, recv_sem, band, sub):
    return pltpu.make_async_remote_copy(
        src_ref=src,
        dst_ref=dst,
        send_sem=send_sem,
        recv_sem=recv_sem,
        device_id=(band, sub),
        device_id_type=pl.DeviceIdType.MESH,
    )


def greet(band, sub):
    pl.semaphore_signal(
        pltpu.get_barrier_semaphore(),
        inc=1,
        device_id=(band, sub),
        device_id_type=pl.DeviceIdType.MESH,
    )


def edge_kernel(
    bands,
    subs,
    capacity,
    slot_ref,
    latent_ref,
    weighted_ref,
    block_ref,
    edge_ref,
    w_mesh_ref,
    w_grid_ref,
    w_msg_ref,
    w_out_ref,
    node_ref,
    outer_ref,
    inner_ref,
    rows_out,
    grads_out,
    rows_in,
    grads_in,
    table,
    proj,
    edge_in,
    index_cols,
    act_weight,
    hot,
    pre,
    grid_part,
    act_grad,
    act_sum,
    pre_grad,
    grid_grad,
    node_acc,
    grid_acc,
    out_acc,
    node_out,
    node_in,
    node_sum,
    node_last,
    node_half,
    node_far,
    outer_parts,
    outer_in,
    outer_near,
    outer_line,
    inner_parts,
    inner_in,
    inner_near,
    inner_line,
    rows_send,
    rows_recv,
    grads_send,
    grads_recv,
    half_send,
    pair_send,
    twin_send,
    table_recv,
    edge_send,
    edge_recv,
    node_send,
    node_recv,
    last_send,
    last_recv,
    far_send,
    far_recv,
    swap_send,
    swap_recv,
    near_send,
    near_recv,
    line_send,
    line_recv,
    back_send,
    back_recv,
    wide_send,
    wide_recv,
    pass_send,
    pass_recv,
):
    lows = bands // HALVES
    pairs = subs // 2
    nears = 2 * pairs
    lines = bands // 2
    padded = rows_out.shape[2]
    block_rows, width = block_ref.shape
    patch = subs * block_rows
    points = latent_ref.shape[0]
    band, sub = lax.axis_index("band"), lax.axis_index("sub")
    half, low = band // lows, band % lows
    pair, parity = sub // 2, sub % 2
    other = 1 - parity
    twin = 2 * pair + other
    group = HALVES * subs
    mine = half * subs + sub
    near, line = (band % 2) * pairs + pair, band // 2

    def low_ahead(step):
        return (low // 2 + step // 2) % (lows // 2) * 2 + (low % 2 + step % 2) % 2

    def low_behind(step):
        return (low // 2 + lows // 2 - step // 2) % (lows // 2) * 2 + (low % 2 + step % 2) % 2

    def member(step):
        index = (mine + step) % group
        return index // subs, index % subs

    def near_device(index):
        return line * 2 + index // pairs, 2 * (index % pairs) + parity

    def line_device(index):
        return index * 2 + band % 2, sub

    @pl.loop(1, group)
    def _(step):
        other_half, other_sub = member(step)
        greet(other_half * lows + low, other_sub)

    @pl.loop(1, lows)
    def _(step):
        greet(half * lows + low_ahead(step), sub)

    @pl.loop(1, nears)
    def _(step):
        greet(*near_device((near + step) % nears))

    @pl.loop(1, lines)
    def _(step):
        greet(*line_device((line + step) % lines))

    pl.semaphore_wait(
        pltpu.get_barrier_semaphore(), group - 1 + lows - 1 + nears - 1 + lines - 1
    )

    def half_copy(source, target):
        return remote(
            block_ref,
            table.at[source, sub],
            half_send.at[target],
            table_recv.at[source, sub],
            target * lows + low,
            sub,
        )

    def pair_copy(src, source_half, source, target):
        place = 2 * source + parity
        return remote(
            src,
            table.at[source_half, place],
            pair_send.at[source_half, target],
            table_recv.at[source_half, place],
            band,
            2 * target + parity,
        )

    def twin_copy(src, source_half, source):
        return remote(
            src,
            table.at[source_half, source],
            twin_send.at[source_half, source // 2],
            table_recv.at[source_half, source],
            band,
            twin,
        )

    def edge_copy(from_half, from_sub, to_half, to_sub):
        return remote(
            edge_ref.at[to_half, to_sub],
            edge_in.at[from_half, from_sub],
            edge_send.at[to_half, to_sub],
            edge_recv.at[from_half, from_sub],
            to_half * lows + low,
            to_sub,
        )

    for step in range(1, pairs):
        pair_copy(block_ref, half, pair, (pair + step) % pairs).start()
    twin_copy(block_ref, half, sub).start()

    @pl.loop(1, group)
    def _(step):
        other_half, other_sub = member(step)
        edge_copy(half, sub, other_half, other_sub).start()

    for step in range(1, HALVES):
        half_copy(half, (half + step) % HALVES).start()

    def spread(target, part, rows, grads):
        places = lax.broadcasted_iota(jnp.int32, (padded, points), 0)
        places = places + (target * HALVES + part) * padded
        one_hot = jnp.where(places == slot_ref[...], 1.0, 0.0).astype(jnp.bfloat16)
        rows[target, part] = times(one_hot, latent_ref[...]).astype(jnp.bfloat16)
        grads[target, part] = times_transpose(one_hot, weighted_ref[...]).astype(jnp.bfloat16)

    def point_copies(source, target, part):
        return (
            remote(
                rows_out.at[target, part],
                rows_in.at[source, part],
                rows_send.at[target, part],
                rows_recv.at[source, part],
                half * lows + target,
                sub,
            ),
            remote(
                grads_out.at[target, part],
                grads_in.at[source, part],
                grads_send.at[target, part],
                grads_recv.at[source, part],
                half * lows + target,
                sub,
            ),
        )

    def split(count):
        return (half + count // lows) % HALVES, count % lows

    @pl.loop(0, HALVES * lows)
    def _(count):
        part, step = split(count)

        @pl.when(step > 0)
        def _():
            target = low_ahead(step)
            spread(target, part, rows_out, grads_out)
            for copy in point_copies(low, target, part):
                copy.start()

    for part in range(HALVES):
        spread(low, part, rows_in, grads_in)

    table[half, sub] = block_ref[...]
    edge_in[half, sub] = edge_ref[half, sub]
    act_weight[...] = lax.dot_general(
        w_out_ref[...], w_msg_ref[...], (((0,), (1,)), ((), ())), preferred_element_type=jnp.float32
    ).astype(jnp.bfloat16)
    node_acc[...] = jnp.zeros_like(node_acc)
    grid_acc[...] = jnp.zeros_like(grid_acc)
    out_acc[...] = jnp.zeros_like(out_acc)

    def arrived(source_half, source):
        remote(
            block_ref,
            table.at[source_half, source],
            twin_send.at[0, 0],
            table_recv.at[source_half, source],
            band,
            twin,
        ).wait_recv()

    def project(source_half, source):
        rows = pl.ds(pl.multiple_of(source * block_rows, block_rows), block_rows)
        proj[source_half, rows] = times(table[source_half, source], w_mesh_ref[...]).astype(
            jnp.bfloat16
        )

    def pass_pairs(source_half):
        for step in range(1, pairs):
            source = 2 * ((pair + step) % pairs) + parity
            arrived(source_half, source)
            twin_copy(table.at[source_half, source], source_half, source).start()

    def finish_table(source_half):
        for source_pair in range(pairs):
            arrived(source_half, 2 * source_pair + other)

        @pl.loop(0, subs)
        def _(source):
            project(source_half, source)

    pass_pairs(half)

    @pl.loop(1, group)
    def _(step):
        other_half, other_sub = member(step)
        edge_copy(other_half, other_sub, half, sub).wait_recv()

    lanes = index_cols.shape[2]
    count = edge_ref.shape[2]
    for part in range(HALVES):
        total = jnp.zeros((count, lanes), jnp.int32)
        for source in range(subs):
            piece = edge_in[part, source]
            if lanes > LANES:
                piece = jnp.concatenate(
                    [piece, jnp.zeros((count, lanes - LANES), jnp.int32)], axis=1
                )
            if source:
                piece = pltpu.roll(piece, source * capacity, 1)
            total = total + piece
        if count < LANES:
            total = jnp.concatenate([total, jnp.zeros((LANES - count, lanes), jnp.int32)], axis=0)
        flipped = total.T
        for source in range(lows):
            moved = pltpu.roll(flipped, LANES - 3 * source, 1) if source else flipped
            index_cols[source, part] = moved

    finish_table(half)

    def process(source, part):
        for corner in range(3):
            column = index_cols[source, part, 0:padded, corner : corner + 1]
            nodes = lax.broadcasted_iota(jnp.int32, (padded, patch), 1)
            hot[corner * padded : (corner + 1) * padded, :] = jnp.where(
                nodes == column, 1.0, 0.0
            ).astype(jnp.bfloat16)
        pre[...] = times(hot[...], proj[part])
        grid_part[...] = times(rows_in[source, part], w_grid_ref[...]).astype(jnp.bfloat16)
        act_grad[...] = times(grads_in[source, part], act_weight[...])

        @pl.loop(0, padded // TILE)
        def _(tile):
            start = pl.multiple_of(tile * TILE, TILE)
            rows = pl.ds(start, TILE)
            base = grid_part[rows].astype(jnp.float32)
            upper = act_grad[rows]
            acts, grads = None, None
            for corner in range(3):
                place = pl.ds(pl.multiple_of(corner * padded + start, TILE), TILE)
                value = pre[place] + base
                sigma = 0.5 * jnp.tanh(0.5 * value) + 0.5
                act = value * sigma
                grad = (upper * (sigma + act * (1.0 - sigma))).astype(jnp.bfloat16)
                pre_grad[place] = grad
                grad = grad.astype(jnp.float32)
                acts = act if acts is None else acts + act
                grads = grad if grads is None else grads + grad
            act_sum[rows] = acts.astype(jnp.bfloat16)
            grid_grad[rows] = grads.astype(jnp.bfloat16)

        out_acc[...] += contract_rows(act_sum[...], grads_in[source, part])
        grid_acc[...] += contract_rows(rows_in[source, part], grid_grad[...])
        node_acc[part] += contract_rows(hot[...], pre_grad[...])

    def node_copies(part):
        return [
            remote(
                node_out.at[part, 2 * index + other],
                node_in.at[part, index],
                node_send.at[part, index],
                node_recv.at[part, index],
                band,
                twin,
            )
            for index in range(pairs)
        ]

    def last_copy(part, source, target):
        return remote(
            node_sum.at[part, target],
            node_last.at[part, source],
            last_send.at[part, target],
            last_recv.at[part, source],
            band,
            2 * target + parity,
        )

    def far_copy(source, target):
        return remote(
            node_half.at[target],
            node_far.at[source],
            far_send.at[target],
            far_recv.at[source],
            target * lows + low,
            sub,
        )

    def add_node(part, index):
        return node_out[part, 2 * index + parity].astype(jnp.float32) + node_in[
            part, index
        ].astype(jnp.float32)

    def swap_nodes(part):
        for source in range(subs):
            rows = pl.ds(source * block_rows, block_rows)
            node_out[part, source] = node_acc[part, rows].astype(jnp.bfloat16)
        for copy in node_copies(part):
            copy.start()

    def send_nodes(part):
        for copy in node_copies(part):
            copy.wait()
        for step in range(1, pairs):
            target = (pair + step) % pairs
            node_sum[part, target] = add_node(part, target).astype(jnp.bfloat16)
            last_copy(part, pair, target).start()

    def gather_node(part):
        running = add_node(part, pair)
        for step in range(1, pairs):
            source = (pair + pairs - step) % pairs
            last_copy(part, source, source).wait_recv()
            running = running + node_last[part, source].astype(jnp.float32)
        return running

    @pl.loop(0, HALVES * lows)
    def _(count):
        part, step = split(count)
        source = low_behind(step)

        @pl.when(count == lows // 2)
        def _():
            for turn in range(1, HALVES):
                source_half = (half + turn) % HALVES
                arrived(source_half, sub)
                place = table.at[source_half, sub]
                twin_copy(place, source_half, sub).start()
                for index in range(1, pairs):
                    pair_copy(place, source_half, pair, (pair + index) % pairs).start()

        @pl.when(count == lows - 1)
        def _():
            for turn in range(1, HALVES):
                pass_pairs((half + turn) % HALVES)

        @pl.when(count == lows)
        def _():
            for turn in range(1, HALVES):
                finish_table((half + turn) % HALVES)
            swap_nodes(half)

        @pl.when(count == lows + 1)
        def _():
            send_nodes(half)

        @pl.when(step > 0)
        def _():
            for copy in point_copies(source, source, part):
                copy.wait_recv()

        process(source, part)

    for turn in range(1, HALVES):
        swap_nodes((half + turn) % HALVES)

    chunks = (
        (outer_parts, outer_in, outer_near, outer_line, outer_ref),
        (inner_parts, inner_in, inner_near, inner_line, inner_ref),
    )

    def swap_copy(index):
        parts, arriving = chunks[index][:2]
        return remote(
            parts.at[other], arriving, swap_send.at[index], swap_recv.at[index], band, twin
        )

    def near_copy(index, source, target):
        parts, _, arriving = chunks[index][:3]
        return remote(
            parts.at[parity, target],
            arriving.at[source],
            near_send.at[index, target],
            near_recv.at[index, source],
            *near_device(target),
        )

    def line_copy(index, source, target):
        parts, _, _, arriving = chunks[index][:4]
        return remote(
            parts.at[parity, near, target],
            arriving.at[source],
            line_send.at[index, target],
            line_recv.at[index, source],
            *line_device(target),
        )

    def back_copy(index, source, target):
        place = chunks[index][4].at[parity, near, source]
        return remote(
            place,
            place,
            back_send.at[index, target],
            back_recv.at[index, source],
            *line_device(target),
        )

    def wide_copy(index, source, target):
        place = chunks[index][4].at[parity, source]
        return remote(
            place,
            place,
            wide_send.at[index, target],
            wide_recv.at[index, source],
            *near_device(target),
        )

    def pass_copy(index, source, side):
        place = chunks[index][4].at[side, source]
        return remote(
            place, place, pass_send.at[index, source], pass_recv.at[index, source], band, twin
        )

    rows = outer_parts.shape[3]

    def fill(parts, value, first):
        for device in range(nears * lines * 2):
            place = (device // (nears * lines), device // lines % nears, device % lines)
            piece = value[device * rows : (device + 1) * rows]
            parts[place + (slice(None), slice(first, first + value.shape[1]))] = piece.astype(
                jnp.bfloat16
            )

    fill(outer_parts, grid_acc[...], 0)
    fill(outer_parts, out_acc[...], width)
    swap_copy(0).start()
    mesh_total = None
    for part in range(HALVES):
        for source in range(subs):
            term = contract_rows(table[part, source], node_out[part, source])
            mesh_total = term if mesh_total is None else mesh_total + term
    fill(inner_parts, mesh_total, 0)
    swap_copy(1).start()

    for turn in range(1, HALVES):
        send_nodes((half + turn) % HALVES)

    def add_up(left, right):
        return (left.astype(jnp.float32) + right.astype(jnp.float32)).astype(jnp.bfloat16)

    for index, (parts, arriving, _, _, _) in enumerate(chunks):
        swap_copy(index).wait()

        @pl.loop(1, nears)
        def _(step):
            target = (near + step) % nears
            parts[parity, target] = add_up(parts[parity, target], arriving[target])
            near_copy(index, near, target).start()

    for turn in range(1, HALVES):
        target = (half + turn) % HALVES
        node_half[target] = gather_node(target).astype(jnp.bfloat16)
        far_copy(half, target).start()

    for index, (parts, arriving, close, _, _) in enumerate(chunks):

        def take_near(step, running):
            source = (near + nears - step) % nears
            near_copy(index, source, source).wait_recv()
            return running + close[source].astype(jnp.float32)

        running = parts[parity, near].astype(jnp.float32) + arriving[near].astype(jnp.float32)
        for step in range(1, nears):
            running = take_near(step, running)
        parts[parity, near] = running.astype(jnp.bfloat16)

        @pl.loop(1, lines)
        def _(step):
            line_copy(index, line, (line + step) % lines).start()

    for index, (parts, _, _, arriving, total) in enumerate(chunks):

        def take_line(step, running):
            source = (line + lines - step) % lines
            line_copy(index, source, source).wait_recv()
            return running + arriving[source].astype(jnp.float32)

        running = parts[parity, near, line].astype(jnp.float32)
        running = lax.fori_loop(1, lines, take_line, running)
        total[parity, near, line] = running.astype(jnp.bfloat16)

        @pl.loop(1, lines)
        def _(step):
            back_copy(index, line, (line + step) % lines).start()

    for index in range(2):

        @pl.loop(1, lines)
        def _(step):
            source = (line + lines - step) % lines
            back_copy(index, source, source).wait_recv()

        @pl.loop(1, nears)
        def _(step):
            wide_copy(index, near, (near + step) % nears).start()

        pass_copy(index, near, parity).start()

    running = gather_node(half)
    for turn in range(1, HALVES):
        source = (half + HALVES - turn) % HALVES
        far_copy(source, source).wait_recv()
        running = running + node_far[source].astype(jnp.float32)
    node_ref[...] = times_transpose(running.astype(jnp.bfloat16), w_mesh_ref[...]).astype(
        jnp.bfloat16
    )

    for index in range(2):

        @pl.loop(1, nears)
        def _(step):
            source = (near + nears - step) % nears
            wide_copy(index, source, source).wait_recv()
            pass_copy(index, source, parity).start()

    for index in range(2):

        @pl.loop(0, nears)
        def _(source):
            pass_copy(index, source, other).wait_recv()
            pass_copy(index, source, parity).wait_send()

        @pl.loop(1, nears)
        def _(step):
            near_copy(index, near, (near + step) % nears).wait_send()
            wide_copy(index, near, (near + step) % nears).wait_send()

        @pl.loop(1, lines)
        def _(step):
            line_copy(index, line, (line + step) % lines).wait_send()
            back_copy(index, line, (line + step) % lines).wait_send()

    @pl.loop(0, HALVES * lows)
    def _(count):
        part, step = split(count)

        @pl.when(step > 0)
        def _():
            for copy in point_copies(low, low_ahead(step), part):
                copy.wait_send()

    for step in range(1, HALVES):
        half_copy(half, (half + step) % HALVES).wait_send()
        far_copy(half, (half + step) % HALVES).wait_send()
    for source_half in range(HALVES):
        for step in range(1, pairs):
            pair_copy(block_ref, source_half, pair, (pair + step) % pairs).wait_send()
            last_copy(source_half, pair, (pair + step) % pairs).wait_send()
        for source_pair in range(pairs):
            twin_copy(block_ref, source_half, 2 * source_pair + parity).wait_send()

    @pl.loop(1, group)
    def _(step):
        other_half, other_sub = member(step)
        edge_copy(half, sub, other_half, other_sub).wait_send()


def edge_pass(slots, latent, weighted, block, edges, w_mesh, w_grid, w_msg, w_out, capacity):
    bands, subs = lax.axis_size("band"), lax.axis_size("sub")
    lows, pairs = bands // HALVES, subs // 2
    nears, lines = 2 * pairs, bands // 2
    padded = round_up(subs * capacity, TILE)
    block_rows, width = block.shape
    patch = subs * block_rows
    columns = weighted.shape[0]
    lanes = round_up(padded, LANES)
    rows = width // (2 * nears * lines)
    vmem = pl.BlockSpec(memory_space=pltpu.VMEM)
    dma = pltpu.SemaphoreType.DMA
    half, full = jnp.bfloat16, jnp.float32

    def chunk(size):
        return [
            pltpu.VMEM((2, nears, lines, rows, size), half),
            pltpu.VMEM((nears, lines, rows, size), half),
            pltpu.VMEM((nears, lines, rows, size), half),
            pltpu.VMEM((lines, rows, size), half),
        ]

    return pl.pallas_call(
        functools.partial(edge_kernel, bands, subs, capacity),
        out_shape=(
            jax.ShapeDtypeStruct((block_rows, width), half),
            jax.ShapeDtypeStruct((2, nears, lines, rows, width + columns), half),
            jax.ShapeDtypeStruct((2, nears, lines, rows, width), half),
        ),
        in_specs=[vmem] * 9,
        out_specs=(vmem, vmem, vmem),
        scratch_shapes=[
            pltpu.VMEM((lows, HALVES, padded, width), half),
            pltpu.VMEM((lows, HALVES, padded, columns), half),
            pltpu.VMEM((lows, HALVES, padded, width), half),
            pltpu.VMEM((lows, HALVES, padded, columns), half),
            pltpu.VMEM((HALVES, subs, block_rows, width), half),
            pltpu.VMEM((HALVES, patch, width), half),
            pltpu.VMEM(edges.shape, jnp.int32),
            pltpu.VMEM((lows, HALVES, lanes, LANES), jnp.int32),
            pltpu.VMEM((columns, width), half),
            pltpu.VMEM((3 * padded, patch), half),
            pltpu.VMEM((3 * padded, width), full),
            pltpu.VMEM((padded, width), half),
            pltpu.VMEM((padded, width), full),
            pltpu.VMEM((padded, width), half),
            pltpu.VMEM((3 * padded, width), half),
            pltpu.VMEM((padded, width), half),
            pltpu.VMEM((HALVES, patch, width), full),
            pltpu.VMEM((width, width), full),
            pltpu.VMEM((width, columns), full),
            pltpu.VMEM((HALVES, subs, block_rows, width), half),
        ]
        + [pltpu.VMEM((HALVES, pairs, block_rows, width), half)] * 3
        + [pltpu.VMEM((HALVES, block_rows, width), half)] * 2
        + chunk(width + columns)
        + chunk(width)
        + [dma((lows, HALVES))] * 4
        + [
            dma((HALVES,)),
            dma((HALVES, pairs)),
            dma((HALVES, pairs)),
            dma((HALVES, subs)),
            dma((HALVES, subs)),
            dma((HALVES, subs)),
        ]
        + [dma((HALVES, pairs))] * 4
        + [dma((HALVES,))] * 2
        + [dma((2,))] * 2
        + [dma((2, nears))] * 2
        + [dma((2, lines))] * 4
        + [dma((2, nears))] * 4,
        compiler_params=pltpu.CompilerParams(
            collective_id=0, has_side_effects=True, vmem_limit_bytes=64000000
        ),
    )(slots, latent, weighted, block, edges, w_mesh, w_grid, w_msg, w_out)


def shards(grad_pred, grid_latent, mesh_latent, send_slot, edge_src, w_mesh, w_grid, w_msg, w_out):
    both = ("band", "sub")
    grid_rows, width = grid_latent.shape
    channels = grad_pred.shape[0]
    bands, subs = lax.axis_size("band"), lax.axis_size("sub")
    devices = bands * subs
    lows = bands // HALVES
    block_rows = mesh_latent.shape[0]
    capacity = 3 * grid_rows // devices
    padded = round_up(subs * capacity, TILE)
    total_points = grid_rows * devices
    own_index = lax.axis_index(both)
    points = own_index * grid_rows + jnp.arange(grid_rows, dtype=jnp.int32)
    weighted = (
        latitude_weight(points, total_points)[None, :] * grad_pred.astype(jnp.float32)
    ).astype(jnp.bfloat16)
    padding = -channels % LANES
    weighted = jnp.pad(weighted, ((0, padding), (0, 0)))
    w_out = jnp.pad(w_out, ((0, 0), (0, padding)))
    holder, rank = send_slot // capacity, send_slot % capacity
    holder_band, holder_sub = holder // subs, holder % subs
    holder_half, holder_low = holder_band // lows, holder_band % lows
    slots = (holder_low * HALVES + holder_half) * padded + holder_sub * capacity + rank
    local = edge_src - lax.axis_index("band") * (subs * block_rows)
    local = local.reshape(3, HALVES, lows, subs, capacity).transpose(1, 3, 2, 0, 4)
    local = local.reshape(HALVES, subs, 3 * lows, capacity)
    local = jnp.pad(local, ((0, 0), (0, 0), (0, -3 * lows % 8), (0, LANES - capacity)))
    mesh_grad, outer, inner = edge_pass(
        slots[None, :],
        grid_latent,
        weighted,
        mesh_latent,
        local,
        w_mesh,
        w_grid,
        w_msg,
        w_out,
        capacity,
    )
    grad_scale = 1.0 / math.sqrt(3.0 * total_points)
    outer = outer.reshape(width, outer.shape[-1])
    inner = inner.reshape(width, width)
    channel_part = outer[:, width:]
    return (
        mesh_grad,
        inner.astype(jnp.float32) * grad_scale,
        outer[:, :width].astype(jnp.float32) * grad_scale,
        times_transpose(channel_part, w_out) * grad_scale,
        contract_rows(w_msg, channel_part[:, :channels]) * grad_scale,
    )


def solution(mesh):
    placed = (
        P(None, ("band", "sub")),
        P(("band", "sub"), None),
        P(("band", "sub"), None),
        P(("band", "sub")),
        P(None, ("band", "sub")),
        P(),
        P(),
        P(),
        P(),
    )
    return jax.shard_map(
        shards,
        mesh=mesh,
        in_specs=placed,
        out_specs=(P(("band", "sub"), None), P(), P(), P(), P()),
        check_vma=False,
    )
```

time: 147 us -> 127 us (0.86)
  the two profiles are of different devices: /device:TPU:15 before, /device:TPU:0 now
where the time goes in v1:
time: 127 us
  Pallas kernels  115 us (91%)
  local copies, waits for them, and re-layouts  4.21 us (3%)
  matrix products  3.4 us (3%)
  other arithmetic  3.07 us (2%)
    pallas_call x1, Pallas kernels, edge_pass(): pl.pallas_call(functools.partial(edge_kernel, bands, subs, capacity), out...  115 us

profile of v1, /device:TPU:0, one launch (start us, length us, event | category | flops | bytes accessed | tf_op | source)
XLA Modules:
  0.0 126.5 jit_solution(13822418512913345305)
XLA Ops:
  0.6 0.0 copy-start.6
  0.7 0.7 fusion.7
  1.4 0.6 broadcast_in_dim.4.slot_ref
  2.0 0.0 copy-done.6
  2.0 0.0 copy-start.5
  2.0 0.1 reshape.34
  2.2 0.6 pad.13.edge_ref
  2.8 0.1 copy-done.5
  3.0 0.1 copy.18
  3.1 0.0 copy-start.3
  3.1 0.7 pad.14.w_out_ref
  3.8 0.3 copy-done.3
  4.2 0.1 multiply_convert_fusion
  4.2 0.8 pad.12.weighted_ref
  5.0 0.0 copy-start
  5.0 115.1 %shard_map.128 = (bf16[320,512]{1,0:T(8,128)(2,1)}, bf16[2,4,4,16,768]{4,3,2,1,0:T(8,128)(2,1)}, bf16[2,4,4,16,512]{4,3,2,1,0:T(8,128)(2,1)}) custom-call(s32[1,768]{1,0:T(1,128)} %broadcast_in_dim.4.slot_ref, bf16[768,512]{1,0:T(8,128)(2,1)} %latent_ref.1, bf16[256,768]{1,0:T(8,128)(2,1)} %pad.12.weighted_ref, bf16[320,512]{1,0:T(8,128)(2,1)} %block_ref.1, ...), custom_call_target="tpu_custom_call" | custom-call | tf_op jit(solution)/shard_map/pallas_call | solution.py:717
  120.2 0.0 copy-start.1
  120.2 0.0 copy-done
  120.2 2.1 %fusion = f32[512,227]{0,1:T(8,128)} fusion(bf16[512,512]{1,0:T(8,128)(2,1)S(1)} %copy-done, bf16[512,768]{1,0:T(8,128)(2,1)} %bitcast.8), kind=kOutput, calls=%fused_computation.2 | convolution fusion | flops 119129600 | bytes 1251328 | tf_op jit(solution)/shard_map/dot_general | solution.py:22
  122.3 0.0 copy-done.1
  122.3 1.3 %convolution_multiply_fusion = f32[512,512]{1,0:T(8,128)} fusion(bf16[512,768]{1,0:T(8,128)(2,1)S(1)} %bitcast.9, bf16[512,227]{1,0:T(8,128)(2,1)S(1)} %copy.18), kind=kOutput, calls=%fused_computation | convolution fusion | flops 134479872 | bytes 1572864 | tf_op jit(solution)/shard_map/dot_general | solution.py:28
  123.6 0.0 copy-start.2
  123.6 1.1 convert_multiply_fusion
  124.7 0.0 copy-done.2
  124.7 0.0 copy-start.4
  124.7 1.1 convert_multiply_fusion.1
  125.8 0.0 copy-done.4
  125.8 0.7 copy.20
  (4 shorter events, 0.1 us)
Async XLA Ops:
  0.6 1.4 %copy-start.6 = (s32[3,2304]{1,0:T(4,128)S(1)}, s32[3,2304]{1,0:T(4,128)}, u32[]{:S(2)}) copy-start(s32[3,2304]{1,0:T(4,128)} %param.13) | copy-start | bytes 82948
  2.0 0.9 copy-start.5
  3.1 1.1 copy-start.3
  5.0 115.2 %copy-start = (bf16[512,512]{1,0:T(8,128)(2,1)S(1)}, bf16[512,512]{1,0:T(8,128)(2,1)}, u32[]{:S(2)}) copy-start(bf16[512,512]{1,0:T(8,128)(2,1)} %w_msg_ref.1) | copy-start | bytes 1572868
  120.2 2.1 %copy-start.1 = (bf16[2,4,4,16,768]{4,3,2,1,0:T(8,128)(2,1)S(1)}, bf16[2,4,4,16,768]{4,3,2,1,0:T(8,128)(2,1)}, u32[]{:S(2)}) copy-start(bf16[2,4,4,16,768]{4,3,2,1,0:T(8,128)(2,1)} %get-tuple-element.10) | copy-start | bytes 2359300
  123.6 1.1 copy-start.2
  124.7 1.1 copy-start.4

commit v2 on v1

--- a/solution.py
+++ b/solution.py
@@ -11,6 +11,7 @@
 HALVES = 2
 LANES = 128
 TILE = 16
+SPAN = 256
 
 
 def latitude_weight(points, total):
@@ -74,10 +75,11 @@
     node_ref,
     outer_ref,
     inner_ref,
+    cargo,
+    weighted,
+    w_out,
     rows_out,
-    grads_out,
     rows_in,
-    grads_in,
     table,
     proj,
     edge_in,
@@ -109,8 +111,6 @@
     inner_line,
     rows_send,
     rows_recv,
-    grads_send,
-    grads_recv,
     half_send,
     pair_send,
     twin_send,
@@ -243,35 +243,32 @@
     for step in range(1, HALVES):
         half_copy(half, (half + step) % HALVES).start()
 
-    def spread(target, part, rows, grads):
+    channels = weighted_ref.shape[0]
+    weighted[...] = jnp.zeros_like(weighted)
+    weighted[0:channels, :] = weighted_ref[...]
+    cargo[:, 0:width] = latent_ref[...]
+    cargo[:, width:] = weighted[...].astype(jnp.float32).T.astype(jnp.bfloat16)
+
+    def spread(target, part, rows):
         places = lax.broadcasted_iota(jnp.int32, (padded, points), 0)
         places = places + (target * HALVES + part) * padded
         one_hot = jnp.where(places == slot_ref[...], 1.0, 0.0).astype(jnp.bfloat16)
-        rows[target, part] = times(one_hot, latent_ref[...]).astype(jnp.bfloat16)
-        grads[target, part] = times_transpose(one_hot, weighted_ref[...]).astype(jnp.bfloat16)
-
-    def point_copies(source, target, part):
-        return (
-            remote(
-                rows_out.at[target, part],
-                rows_in.at[source, part],
-                rows_send.at[target, part],
-                rows_recv.at[source, part],
-                half * lows + target,
-                sub,
-            ),
-            remote(
-                grads_out.at[target, part],
-                grads_in.at[source, part],
-                grads_send.at[target, part],
-                grads_recv.at[source, part],
-                half * lows + target,
-                sub,
-            ),
+        rows[target, part] = times(one_hot, cargo[...]).astype(jnp.bfloat16)
+
+    def point_copy(source, target, part):
+        return remote(
+            rows_out.at[target, part],
+            rows_in.at[source, part],
+            rows_send.at[target, part],
+            rows_recv.at[source, part],
+            half * lows + target,
+            sub,
         )
 
     def split(count):
-        return (half + count // lows) % HALVES, count % lows
+        block = lows // 2
+        turn = (count // block + 1) // 2
+        return (half + turn) % HALVES, count - block * turn
 
     @pl.loop(0, HALVES * lows)
     def _(count):
@@ -280,17 +277,18 @@
         @pl.when(step > 0)
         def _():
             target = low_ahead(step)
-            spread(target, part, rows_out, grads_out)
-            for copy in point_copies(low, target, part):
-                copy.start()
+            spread(target, part, rows_out)
+            point_copy(low, target, part).start()
 
     for part in range(HALVES):
-        spread(low, part, rows_in, grads_in)
+        spread(low, part, rows_in)
 
     table[half, sub] = block_ref[...]
     edge_in[half, sub] = edge_ref[half, sub]
-    act_weight[...] = lax.dot_general(
-        w_out_ref[...], w_msg_ref[...], (((0,), (1,)), ((), ())), preferred_element_type=jnp.float32
+    w_out[...] = jnp.zeros_like(w_out)
+    w_out[:, 0:channels] = w_out_ref[...]
+    act_weight[...] = 0.5 * lax.dot_general(
+        w_out[...], w_msg_ref[...], (((0,), (1,)), ((), ())), preferred_element_type=jnp.float32
     ).astype(jnp.bfloat16)
     node_acc[...] = jnp.zeros_like(node_acc)
     grid_acc[...] = jnp.zeros_like(grid_acc)
@@ -308,9 +306,9 @@
 
     def project(source_half, source):
         rows = pl.ds(pl.multiple_of(source * block_rows, block_rows), block_rows)
-        proj[source_half, rows] = times(table[source_half, source], w_mesh_ref[...]).astype(
-            jnp.bfloat16
-        )
+        proj[source_half, rows] = 0.5 * times(
+            table[source_half, source], w_mesh_ref[...]
+        ).astype(jnp.bfloat16)
 
     def pass_pairs(source_half):
         for step in range(1, pairs):
@@ -355,40 +353,65 @@
 
     finish_table(half)
 
-    def process(source, part):
+    for turn in range(1, HALVES):
+        source_half = (half + turn) % HALVES
+        arrived(source_half, sub)
+        place = table.at[source_half, sub]
+        twin_copy(place, source_half, sub).start()
+        for index in range(1, pairs):
+            pair_copy(place, source_half, pair, (pair + index) % pairs).start()
+
+    def scatter(count, block):
+        part, _ = split(count)
+        slot = count % 2
+        nodes = slice(block * SPAN, (block + 1) * SPAN)
+        node_acc[part, nodes] += contract_rows(hot[slot, :, nodes], pre_grad[slot])
+
+    def process(count, scattered):
+        part, step = split(count)
+        source = low_behind(step)
+        slot = count % 2
         for corner in range(3):
             column = index_cols[source, part, 0:padded, corner : corner + 1]
             nodes = lax.broadcasted_iota(jnp.int32, (padded, patch), 1)
-            hot[corner * padded : (corner + 1) * padded, :] = jnp.where(
+            hot[slot, corner * padded : (corner + 1) * padded, :] = jnp.where(
                 nodes == column, 1.0, 0.0
             ).astype(jnp.bfloat16)
-        pre[...] = times(hot[...], proj[part])
-        grid_part[...] = times(rows_in[source, part], w_grid_ref[...]).astype(jnp.bfloat16)
-        act_grad[...] = times(grads_in[source, part], act_weight[...])
-
-        @pl.loop(0, padded // TILE)
-        def _(tile):
-            start = pl.multiple_of(tile * TILE, TILE)
+        latents = rows_in[source, part, :, 0:width]
+        losses = rows_in[source, part, :, width:]
+        pre[...] = times(hot[slot], proj[part])
+        grid_part[...] = 0.5 * times(latents, w_grid_ref[...]).astype(jnp.bfloat16)
+        act_grad[...] = times(losses, act_weight[...])
+
+        def finish(start):
             rows = pl.ds(start, TILE)
             base = grid_part[rows].astype(jnp.float32)
             upper = act_grad[rows]
             acts, grads = None, None
             for corner in range(3):
-                place = pl.ds(pl.multiple_of(corner * padded + start, TILE), TILE)
+                place = pl.ds(corner * padded + start, TILE)
                 value = pre[place] + base
-                sigma = 0.5 * jnp.tanh(0.5 * value) + 0.5
-                act = value * sigma
-                grad = (upper * (sigma + act * (1.0 - sigma))).astype(jnp.bfloat16)
-                pre_grad[place] = grad
-                grad = grad.astype(jnp.float32)
+                tanh = jnp.tanh(value)
+                above = 1.0 + tanh
+                act = value * above
+                grad = upper * (above + act * (1.0 - tanh))
+                pre_grad[slot, place] = grad.astype(jnp.bfloat16)
                 acts = act if acts is None else acts + act
                 grads = grad if grads is None else grads + grad
             act_sum[rows] = acts.astype(jnp.bfloat16)
             grid_grad[rows] = grads.astype(jnp.bfloat16)
 
-        out_acc[...] += contract_rows(act_sum[...], grads_in[source, part])
-        grid_acc[...] += contract_rows(rows_in[source, part], grid_grad[...])
-        node_acc[part] += contract_rows(hot[...], pre_grad[...])
+        tiles = padded // TILE
+        blocks = patch // SPAN
+        done = 0
+        for tile in range(tiles):
+            while scattered and done * tiles < (tile + 1) * blocks:
+                scatter(count - 1, done)
+                done += 1
+            finish(tile * TILE)
+
+        out_acc[...] += contract_rows(act_sum[...], losses)
+        grid_acc[...] += contract_rows(latents, grid_grad[...])
 
     def node_copies(part):
         return [
@@ -451,7 +474,9 @@
             running = running + node_last[part, source].astype(jnp.float32)
         return running
 
-    @pl.loop(0, HALVES * lows)
+    process(0, False)
+
+    @pl.loop(1, HALVES * lows)
     def _(count):
         part, step = split(count)
         source = low_behind(step)
@@ -459,37 +484,19 @@
         @pl.when(count == lows // 2)
         def _():
             for turn in range(1, HALVES):
-                source_half = (half + turn) % HALVES
-                arrived(source_half, sub)
-                place = table.at[source_half, sub]
-                twin_copy(place, source_half, sub).start()
-                for index in range(1, pairs):
-                    pair_copy(place, source_half, pair, (pair + index) % pairs).start()
-
-        @pl.when(count == lows - 1)
+                pass_pairs((half + turn) % HALVES)
+                finish_table((half + turn) % HALVES)
+
+        @pl.when(count == lows // 2 + lows + 1)
         def _():
             for turn in range(1, HALVES):
-                pass_pairs((half + turn) % HALVES)
-
-        @pl.when(count == lows)
-        def _():
-            for turn in range(1, HALVES):
-                finish_table((half + turn) % HALVES)
-            swap_nodes(half)
-
-        @pl.when(count == lows + 1)
-        def _():
-            send_nodes(half)
+                swap_nodes((half + turn) % HALVES)
 
         @pl.when(step > 0)
         def _():
-            for copy in point_copies(source, source, part):
-                copy.wait_recv()
-
-        process(source, part)
-
-    for turn in range(1, HALVES):
-        swap_nodes((half + turn) % HALVES)
+            point_copy(source, source, part).wait_recv()
+
+        process(count, True)
 
     chunks = (
         (outer_parts, outer_in, outer_near, outer_line, outer_ref),
@@ -561,6 +568,11 @@
     fill(outer_parts, grid_acc[...], 0)
     fill(outer_parts, out_acc[...], width)
     swap_copy(0).start()
+    for turn in range(1, HALVES):
+        send_nodes((half + turn) % HALVES)
+    for block in range(patch // SPAN):
+        scatter(HALVES * lows - 1, block)
+    swap_nodes(half)
     mesh_total = None
     for part in range(HALVES):
         for source in range(subs):
@@ -569,13 +581,11 @@
     fill(inner_parts, mesh_total, 0)
     swap_copy(1).start()
 
-    for turn in range(1, HALVES):
-        send_nodes((half + turn) % HALVES)
-
     def add_up(left, right):
         return (left.astype(jnp.float32) + right.astype(jnp.float32)).astype(jnp.bfloat16)
 
-    for index, (parts, arriving, _, _, _) in enumerate(chunks):
+    def start_near(index):
+        parts, arriving = chunks[index][:2]
         swap_copy(index).wait()
 
         @pl.loop(1, nears)
@@ -584,10 +594,13 @@
             parts[parity, target] = add_up(parts[parity, target], arriving[target])
             near_copy(index, near, target).start()
 
+    start_near(0)
     for turn in range(1, HALVES):
         target = (half + turn) % HALVES
         node_half[target] = gather_node(target).astype(jnp.bfloat16)
         far_copy(half, target).start()
+    start_near(1)
+    send_nodes(half)
 
     for index, (parts, arriving, close, _, _) in enumerate(chunks):
 
@@ -673,8 +686,7 @@
 
         @pl.when(step > 0)
         def _():
-            for copy in point_copies(low, low_ahead(step), part):
-                copy.wait_send()
+            point_copy(low, low_ahead(step), part).wait_send()
 
     for step in range(1, HALVES):
         half_copy(half, (half + step) % HALVES).wait_send()
@@ -699,7 +711,7 @@
     padded = round_up(subs * capacity, TILE)
     block_rows, width = block.shape
     patch = subs * block_rows
-    columns = weighted.shape[0]
+    columns = round_up(weighted.shape[0], LANES)
     lanes = round_up(padded, LANES)
     rows = width // (2 * nears * lines)
     vmem = pl.BlockSpec(memory_space=pltpu.VMEM)
@@ -724,21 +736,22 @@
         in_specs=[vmem] * 9,
         out_specs=(vmem, vmem, vmem),
         scratch_shapes=[
-            pltpu.VMEM((lows, HALVES, padded, width), half),
-            pltpu.VMEM((lows, HALVES, padded, columns), half),
-            pltpu.VMEM((lows, HALVES, padded, width), half),
-            pltpu.VMEM((lows, HALVES, padded, columns), half),
+            pltpu.VMEM((latent.shape[0], width + columns), half),
+            pltpu.VMEM((columns, latent.shape[0]), half),
+            pltpu.VMEM((width, columns), half),
+            pltpu.VMEM((lows, HALVES, padded, width + columns), half),
+            pltpu.VMEM((lows, HALVES, padded, width + columns), half),
             pltpu.VMEM((HALVES, subs, block_rows, width), half),
             pltpu.VMEM((HALVES, patch, width), half),
             pltpu.VMEM(edges.shape, jnp.int32),
             pltpu.VMEM((lows, HALVES, lanes, LANES), jnp.int32),
             pltpu.VMEM((columns, width), half),
-            pltpu.VMEM((3 * padded, patch), half),
+            pltpu.VMEM((2, 3 * padded, patch), half),
             pltpu.VMEM((3 * padded, width), full),
             pltpu.VMEM((padded, width), half),
             pltpu.VMEM((padded, width), full),
             pltpu.VMEM((padded, width), half),
-            pltpu.VMEM((3 * padded, width), half),
+            pltpu.VMEM((2, 3 * padded, width), half),
             pltpu.VMEM((padded, width), half),
             pltpu.VMEM((HALVES, patch, width), full),
             pltpu.VMEM((width, width), full),
@@ -749,7 +762,7 @@
         + [pltpu.VMEM((HALVES, block_rows, width), half)] * 2
         + chunk(width + columns)
         + chunk(width)
-        + [dma((lows, HALVES))] * 4
+        + [dma((lows, HALVES))] * 2
         + [
             dma((HALVES,)),
             dma((HALVES, pairs)),
@@ -786,9 +799,6 @@
     weighted = (
         latitude_weight(points, total_points)[None, :] * grad_pred.astype(jnp.float32)
     ).astype(jnp.bfloat16)
-    padding = -channels % LANES
-    weighted = jnp.pad(weighted, ((0, padding), (0, 0)))
-    w_out = jnp.pad(w_out, ((0, 0), (0, padding)))
     holder, rank = send_slot // capacity, send_slot % capacity
     holder_band, holder_sub = holder // subs, holder % subs
     holder_half, holder_low = holder_band // lows, holder_band % lows
@@ -817,7 +827,7 @@
         mesh_grad,
         inner.astype(jnp.float32) * grad_scale,
         outer[:, :width].astype(jnp.float32) * grad_scale,
-        times_transpose(channel_part, w_out) * grad_scale,
+        times_transpose(channel_part[:, :channels], w_out) * grad_scale,
         contract_rows(w_msg, channel_part[:, :channels]) * grad_scale,
     )
 

time: 127 us -> 115 us (0.906)
  Pallas kernels: 115 us -> 104 us
  other arithmetic: 3.07 us -> 5.22 us
    pallas_call x1, Pallas kernels: 115 us -> 104 us  [edge_pass(): pl.pallas_call(functools.partial(edge_kernel, bands, subs, capacity), out...]
    convert_element_type x1, other arithmetic: 0.06 us -> 1.79 us  [shards(): weighted = (latitude_weight(points, total_points)[None, :] * grad_pred.as...]
    pad x2 -> x0, local copies, waits for them, and re-layouts: 1.52 us -> none  [the longest x1 0.77 us: shards(): weighted = jnp.pad(weighted, ((0, padding), (0, 0)))]
where the time goes in v2:
time: 115 us
  Pallas kernels  104 us (90%)
  other arithmetic  5.22 us (5%)
  local copies, waits for them, and re-layouts  3.08 us (3%)
  matrix products  2.35 us (2%)
    pallas_call x1, Pallas kernels, edge_pass(): pl.pallas_call(functools.partial(edge_kernel, bands, subs, capacity), out...  104 us

profile of v2, /device:TPU:0, one launch (start us, length us, event | category | flops | bytes accessed | tf_op | source)
XLA Modules:
  0.0 115.2 jit_solution(14968075622197737397)
XLA Ops:
  0.7 0.0 copy-start.5
  0.7 1.8 %multiply_convert_fusion.weighted_ref = bf16[227,768]{1,0:T(8,128)(2,1)} fusion(bf16[227,768]{1,0:T(8,128)(2,1)} %param.9, f32[768]{0:T(1024)S(1)} %cosine_multiply_fusion), kind=kLoop, calls=%fused_computation.5 | loop fusion | flops 523008 | bytes 700416 | tf_op jit(solution)/shard_map/convert_element_type | solution.py:801
  2.5 0.0 copy-done.5
  2.5 0.0 copy-start.2
  2.5 0.1 reshape.34
  2.7 0.6 pad.4.edge_ref
  3.3 0.1 copy-done.2
  3.4 0.0 copy-start.6
  3.4 0.8 copy.18.w_out_ref
  4.3 0.0 copy-done.6
  4.3 0.6 broadcast_in_dim.4.slot_ref
  4.9 103.9 %shard_map.128 = (bf16[320,512]{1,0:T(8,128)(2,1)}, bf16[2,4,4,16,768]{4,3,2,1,0:T(8,128)(2,1)}, bf16[2,4,4,16,512]{4,3,2,1,0:T(8,128)(2,1)}) custom-call(s32[1,768]{1,0:T(1,128)} %broadcast_in_dim.4.slot_ref, bf16[768,512]{1,0:T(8,128)(2,1)} %latent_ref.1, bf16[227,768]{1,0:T(8,128)(2,1)} %multiply_convert_fusion.weighted_ref, bf16[320,512]{1,0:T(8,128)(2,1)} %block_ref.1, ...), custom_call_target="tpu_custom_call" | custom-call | tf_op jit(solution)/shard_map/pallas_call | solution.py:729
  108.8 0.0 copy-start.1
  108.8 2.2 %convert_multiply_fusion = f32[512,512]{1,0:T(8,128)} fusion(bf16[512,768]{1,0:T(8,128)(2,1)} %bitcast.9), kind=kLoop, calls=%fused_computation.3 | loop fusion | flops 524288 | bytes 1572864 | tf_op jit(solution)/shard_map/mul | solution.py:829
  111.0 0.0 copy-done.1
  111.0 0.0 copy-start
  111.0 1.3 %convolution_multiply_fusion = f32[512,512]{1,0:T(8,128)} fusion(bf16[512,227]{0,1:T(8,128)(2,1)S(1)} %copy-done.2, bf16[512,768]{1,0:T(8,128)(2,1)S(1)} %bitcast.10), kind=kOutput, calls=%fused_computation | convolution fusion | flops 119275520 | bytes 1548288 | tf_op jit(solution)/shard_map/dot_general | solution.py:29
  112.3 0.0 copy-done
  112.3 0.0 copy-start.3
  112.3 1.1 fusion
  113.4 0.0 copy-done.3
  113.4 0.0 copy-start.4
  113.4 1.1 convert_multiply_fusion.1
  114.5 0.0 copy-done.4
  114.5 0.7 copy.20
  (5 shorter events, 0.1 us)
Async XLA Ops:
  0.7 1.8 %copy-start.5 = (s32[3,2304]{1,0:T(4,128)S(1)}, s32[3,2304]{1,0:T(4,128)}, u32[]{:S(2)}) copy-start(s32[3,2304]{1,0:T(4,128)} %param.13) | copy-start | bytes 82948
  2.5 0.9 copy-start.2
  3.4 0.8 copy-start.6
  108.8 2.2 %copy-start.1 = (bf16[2,4,4,16,768]{4,3,2,1,0:T(8,128)(2,1)S(1)}, bf16[2,4,4,16,768]{4,3,2,1,0:T(8,128)(2,1)}, u32[]{:S(2)}) copy-start(bf16[2,4,4,16,768]{4,3,2,1,0:T(8,128)(2,1)} %get-tuple-element.10) | copy-start | bytes 2359300
  111.0 1.3 %copy-start = (bf16[512,512]{1,0:T(8,128)(2,1)S(1)}, bf16[512,512]{1,0:T(8,128)(2,1)}, u32[]{:S(2)}) copy-start(bf16[512,512]{1,0:T(8,128)(2,1)} %w_msg_ref.1) | copy-start | bytes 1572868
  112.3 1.1 copy-start.3
  113.4 1.1 copy-start.4

commit v3 on v2

--- a/solution.py
+++ b/solution.py
@@ -231,14 +231,14 @@
             to_sub,
         )
 
-    for step in range(1, pairs):
-        pair_copy(block_ref, half, pair, (pair + step) % pairs).start()
-    twin_copy(block_ref, half, sub).start()
-
     @pl.loop(1, group)
     def _(step):
         other_half, other_sub = member(step)
         edge_copy(half, sub, other_half, other_sub).start()
+
+    for step in range(1, pairs):
+        pair_copy(block_ref, half, pair, (pair + step) % pairs).start()
+    twin_copy(block_ref, half, sub).start()
 
     for step in range(1, HALVES):
         half_copy(half, (half + step) % HALVES).start()
@@ -474,29 +474,49 @@
             running = running + node_last[part, source].astype(jnp.float32)
         return running
 
-    process(0, False)
-
-    @pl.loop(1, HALVES * lows)
-    def _(count):
+    def scatter_all(count):
+        for block in range(patch // SPAN):
+            scatter(count, block)
+
+    def run(count):
         part, step = split(count)
         source = low_behind(step)
-
-        @pl.when(count == lows // 2)
-        def _():
-            for turn in range(1, HALVES):
-                pass_pairs((half + turn) % HALVES)
-                finish_table((half + turn) % HALVES)
-
-        @pl.when(count == lows // 2 + lows + 1)
-        def _():
-            for turn in range(1, HALVES):
-                swap_nodes((half + turn) % HALVES)
 
         @pl.when(step > 0)
         def _():
             point_copy(source, source, part).wait_recv()
 
         process(count, True)
+
+    first = lows // 2
+    last = first + (HALVES - 1) * lows
+
+    process(0, False)
+    @pl.loop(1, first)
+    def _(count):
+        run(count)
+
+    for turn in range(1, HALVES):
+        pass_pairs((half + turn) % HALVES)
+        finish_table((half + turn) % HALVES)
+
+    @pl.loop(first, last)
+    def _(count):
+        run(count)
+
+    scatter_all(last - 1)
+    for turn in range(1, HALVES):
+        swap_nodes((half + turn) % HALVES)
+    part, step = split(last)
+    source = low_behind(step)
+    point_copy(source, source, part).wait_recv()
+    process(last, False)
+    for turn in range(1, HALVES):
+        send_nodes((half + turn) % HALVES)
+
+    @pl.loop(last + 1, HALVES * lows)
+    def _(count):
+        run(count)
 
     chunks = (
         (outer_parts, outer_in, outer_near, outer_line, outer_ref),
@@ -568,11 +588,12 @@
     fill(outer_parts, grid_acc[...], 0)
     fill(outer_parts, out_acc[...], width)
     swap_copy(0).start()
+    scatter_all(HALVES * lows - 1)
+    swap_nodes(half)
     for turn in range(1, HALVES):
-        send_nodes((half + turn) % HALVES)
-    for block in range(patch // SPAN):
-        scatter(HALVES * lows - 1, block)
-    swap_nodes(half)
+        target = (half + turn) % HALVES
+        node_half[target] = gather_node(target).astype(jnp.bfloat16)
+        far_copy(half, target).start()
     mesh_total = None
     for part in range(HALVES):
         for source in range(subs):
@@ -595,10 +616,6 @@
             near_copy(index, near, target).start()
 
     start_near(0)
-    for turn in range(1, HALVES):
-        target = (half + turn) % HALVES
-        node_half[target] = gather_node(target).astype(jnp.bfloat16)
-        far_copy(half, target).start()
     start_near(1)
     send_nodes(half)
 

time: 115 us -> 110 us (0.957)
  Pallas kernels: 104 us -> 98.5 us
    pallas_call x1, Pallas kernels: 104 us -> 98.5 us  [edge_pass(): pl.pallas_call(functools.partial(edge_kernel, bands, subs, capacity), out...]
where the time goes in v3:
time: 110 us
  Pallas kernels  98.5 us (90%)
  other arithmetic  5.22 us (5%)
  local copies, waits for them, and re-layouts  3.08 us (3%)
  matrix products  2.35 us (2%)
    pallas_call x1, Pallas kernels, edge_pass(): pl.pallas_call(functools.partial(edge_kernel, bands, subs, capacity), out...  98.5 us
    mul x1, other arithmetic, shards(): outer[:, :width].astype(jnp.float32) * grad_scale  2.23 us

profile of v3, /device:TPU:0, one launch (start us, length us, event | category | flops | bytes accessed | tf_op | source)
XLA Modules:
  0.0 109.9 jit_solution(8736427000075155135)
XLA Ops:
  0.7 0.0 copy-start.5
  0.7 1.8 %multiply_convert_fusion.weighted_ref = bf16[227,768]{1,0:T(8,128)(2,1)} fusion(bf16[227,768]{1,0:T(8,128)(2,1)} %param.9, f32[768]{0:T(1024)S(1)} %cosine_multiply_fusion), kind=kLoop, calls=%fused_computation.5 | loop fusion | flops 523008 | bytes 700416 | tf_op jit(solution)/shard_map/convert_element_type | solution.py:818
  2.5 0.0 copy-done.5
  2.5 0.0 copy-start.2
  2.5 0.1 reshape.34
  2.7 0.6 pad.4.edge_ref
  3.3 0.1 copy-done.2
  3.4 0.0 copy-start.6
  3.4 0.8 copy.18.w_out_ref
  4.3 0.0 copy-done.6
  4.3 0.6 broadcast_in_dim.4.slot_ref
  4.9 98.5 %shard_map.128 = (bf16[320,512]{1,0:T(8,128)(2,1)}, bf16[2,4,4,16,768]{4,3,2,1,0:T(8,128)(2,1)}, bf16[2,4,4,16,512]{4,3,2,1,0:T(8,128)(2,1)}) custom-call(s32[1,768]{1,0:T(1,128)} %broadcast_in_dim.4.slot_ref, bf16[768,512]{1,0:T(8,128)(2,1)} %latent_ref.1, bf16[227,768]{1,0:T(8,128)(2,1)} %multiply_convert_fusion.weighted_ref, bf16[320,512]{1,0:T(8,128)(2,1)} %block_ref.1, ...), custom_call_target="tpu_custom_call" | custom-call | tf_op jit(solution)/shard_map/pallas_call | solution.py:746
  103.4 0.0 copy-start.1
  103.4 2.2 %convert_multiply_fusion = f32[512,512]{1,0:T(8,128)} fusion(bf16[512,768]{1,0:T(8,128)(2,1)} %bitcast.9), kind=kLoop, calls=%fused_computation.3 | loop fusion | flops 524288 | bytes 1572864 | tf_op jit(solution)/shard_map/mul | solution.py:846
  105.7 0.0 copy-done.1
  105.7 0.0 copy-start
  105.7 1.3 %convolution_multiply_fusion = f32[512,512]{1,0:T(8,128)} fusion(bf16[512,227]{0,1:T(8,128)(2,1)S(1)} %copy-done.2, bf16[512,768]{1,0:T(8,128)(2,1)S(1)} %bitcast.10), kind=kOutput, calls=%fused_computation | convolution fusion | flops 119275520 | bytes 1548288 | tf_op jit(solution)/shard_map/dot_general | solution.py:29
  107.0 0.0 copy-done
  107.0 0.0 copy-start.3
  107.0 1.1 fusion
  108.0 0.0 copy-done.3
  108.0 0.0 copy-start.4
  108.0 1.1 %convert_multiply_fusion.1 = f32[2,4,4,16,512]{4,3,2,1,0:T(8,128)} fusion(bf16[2,4,4,16,512]{4,3,2,1,0:T(8,128)(2,1)S(1)} %copy-done.3), kind=kLoop, calls=%fused_computation.4 | loop fusion | flops 524288 | bytes 1572864 | tf_op jit(solution)/shard_map/mul | solution.py:845
  109.2 0.0 copy-done.4
  109.2 0.7 copy.20
  (5 shorter events, 0.1 us)
Async XLA Ops:
  0.7 1.8 %copy-start.5 = (s32[3,2304]{1,0:T(4,128)S(1)}, s32[3,2304]{1,0:T(4,128)}, u32[]{:S(2)}) copy-start(s32[3,2304]{1,0:T(4,128)} %param.13) | copy-start | bytes 82948
  2.5 0.9 copy-start.2
  3.4 0.8 copy-start.6
  103.4 2.2 %copy-start.1 = (bf16[2,4,4,16,768]{4,3,2,1,0:T(8,128)(2,1)S(1)}, bf16[2,4,4,16,768]{4,3,2,1,0:T(8,128)(2,1)}, u32[]{:S(2)}) copy-start(bf16[2,4,4,16,768]{4,3,2,1,0:T(8,128)(2,1)} %get-tuple-element.10) | copy-start | bytes 2359300
  105.7 1.3 %copy-start = (bf16[512,512]{1,0:T(8,128)(2,1)S(1)}, bf16[512,512]{1,0:T(8,128)(2,1)}, u32[]{:S(2)}) copy-start(bf16[512,512]{1,0:T(8,128)(2,1)} %w_msg_ref.1) | copy-start | bytes 1572868
  107.0 1.1 copy-start.3
  108.0 1.1 %copy-start.4 = (bf16[320,512]{1,0:T(8,128)(2,1)S(1)}, bf16[320,512]{1,0:T(8,128)(2,1)}, u32[]{:S(2)}) copy-start(bf16[320,512]{1,0:T(8,128)(2,1)} %get-tuple-element.16) | copy-start | bytes 983044
